TPU v7x, 32 devices: a whole 2x2x4 slice. The times are simulated.
32 devices in a mesh: seq: 8 (over y, x, core), wshard: 4 (over z).
Axes of the slice: x: 2, y: 2, z: 4, core: 2. Of those that a mesh axis runs over, the one named last changes fastest.
Arguments:
- block_in: bfloat16 [4, 2048, 1536], P('wshard', 'seq'), may hold values from -6 to 6
- cotangent: bfloat16 [4, 2048, 1536], P('wshard', 'seq'), may hold values from -6 to 6
- in_weight: float32 [1536, 6448], P(('seq', 'wshard')), may hold values from -0.15625 to 0.15625
- out_weight: float32 [3072, 1536], P(('seq', 'wshard')), may hold values from -0.109375 to 0.109375
- in_gain: float32 [1536], replicated, may hold values from 0.5 to 1.5
- out_gain: float32 [3072], replicated, may hold values from 0.5 to 1.5
- conv_inner: float32 [5, 3072], replicated, may hold values from -3 to 3
- conv_shared: float32 [5, 256], replicated, may hold values from -3 to 3
- head_params: float32 [3, 48], replicated, may hold values from -5 to 1.5, as said below
- first_in_weight: float32 [1536, 6448], P(('seq', 'wshard')), may hold values from -6 to 6
- first_out_weight: float32 [3072, 1536], P(('seq', 'wshard')), may hold values from -6 to 6
- first_in_gain: float32 [1536], replicated, may hold values from -6 to 6
- first_out_gain: float32 [3072], replicated, may hold values from -6 to 6
- first_conv_inner: float32 [5, 3072], replicated, may hold values from -6 to 6
- first_conv_shared: float32 [5, 256], replicated, may hold values from -6 to 6
- first_head_params: float32 [3, 48], replicated, may hold values from -6 to 6
- second_in_weight: float32 [1536, 6448], P(('seq', 'wshard')), may hold values from 0.01 to 1
- second_out_weight: float32 [3072, 1536], P(('seq', 'wshard')), may hold values from 0.01 to 1
- second_in_gain: float32 [1536], replicated, may hold values from 16.384 to 1638.4
- second_out_gain: float32 [3072], replicated, may hold values from 0.01 to 1
- second_conv_inner: float32 [5, 3072], replicated, may hold values from 0.01 to 1
- second_conv_shared: float32 [5, 256], replicated, may hold values from 0.01 to 1
- second_head_params: float32 [3, 48], replicated, may hold values from 0.01 to 1
Outputs:
- block_out: float32 [4, 2048, 1536], P('wshard', 'seq')
- grad_in: float32 [4, 2048, 1536], P('wshard', 'seq')
- grad_in_weight: float32 [1536, 6448], P(('seq', 'wshard'))
- grad_out_weight: float32 [3072, 1536], P(('seq', 'wshard'))
- grad_in_gain: float32 [1536], replicated
- grad_out_gain: float32 [3072], replicated
- grad_conv_inner: float32 [5, 3072], replicated
- grad_conv_shared: float32 [5, 256], replicated
- grad_head_params: float32 [3, 48], replicated
- new_in_weight: float32 [1536, 6448], P(('seq', 'wshard'))
- new_out_weight: float32 [3072, 1536], P(('seq', 'wshard'))
- updated_input_gain: float32 [1536], replicated
- new_out_gain: float32 [3072], replicated
- new_conv_inner: float32 [5, 3072], replicated
- new_conv_shared: float32 [5, 256], replicated
- new_head_params: float32 [3, 48], replicated
- new_first_in_weight: float32 [1536, 6448], P(('seq', 'wshard'))
- new_first_out_weight: float32 [3072, 1536], P(('seq', 'wshard'))
- new_first_in_gain: float32 [1536], replicated
- new_first_out_gain: float32 [3072], replicated
- new_first_conv_inner: float32 [5, 3072], replicated
- new_first_conv_shared: float32 [5, 256], replicated
- updated_head_first_moment: float32 [3, 48], replicated
- new_second_in_weight: float32 [1536, 6448], P(('seq', 'wshard'))
- new_second_out_weight: float32 [3072, 1536], P(('seq', 'wshard'))
- new_second_in_gain: float32 [1536], replicated
- new_second_out_gain: float32 [3072], replicated
- new_second_conv_inner: float32 [5, 3072], replicated
- new_second_conv_shared: float32 [5, 256], replicated
- new_second_head_params: float32 [2, 48], replicated
- new_second_skip: float32 [48], replicated
Inputs may be any that keep to these rules, and one draw needn't show every extreme that they name: `head_params`: row 0 holds step biases, row 1 logarithms of decay rates, row 2 skip gains.
All inputs are finite; a program needn't handle non-finite values.
Results may differ from a plain program's by a relative error of at most 0.02.
The roundings to bfloat16 on the way count: a program that leaves them out, or rounds other values in their place, can miss the bound.
Values may be sent and summed in bfloat16 or wider, within the bound.
A program may use at most 256 MiB of HBM per device.

v0:
```python
import jax
import jax.numpy as jnp
from jax import lax
from jax.sharding import PartitionSpec as P

P_SIZE = 64
N_STATE = 128
BLOCK_LEN = 256
E = 3072
norm_eps = 1e-05
beta_one = 0.9
beta_two = 0.95
adam_eps = 1e-08
adam_step = 3.0
weight_learning_rate = 0.01
matrix_decay = 0.1
small_rate = 0.1


def causal_conv(values, taps):
    length = values.shape[1]
    width = taps.shape[0] - 1
    padded = jnp.pad(values, ((0, 0), (width - 1, 0), (0, 0)))
    total = taps[width] + taps[0] * padded[:, 0:length]
    for shift in range(1, width):
        total = total + taps[shift] * padded[:, shift : shift + length]
    return total


def block_step(state, inputs):
    inner_part, step_part, learning_rate_piece, b_part, c_part = inputs
    high = lax.Precision.HIGHEST
    cumul = jnp.cumsum(learning_rate_piece, axis=1)
    scores = jnp.einsum("sin,sjn->sij", c_part, b_part, precision=high)
    rows = lax.broadcasted_iota(jnp.int32, (BLOCK_LEN, BLOCK_LEN), 0)
    cols = lax.broadcasted_iota(jnp.int32, (BLOCK_LEN, BLOCK_LEN), 1)
    lower = (rows >= cols)[None, :, :, None]
    spread = cumul[:, :, None, :] - cumul[:, None, :, :]
    decay = jnp.where(lower, jnp.exp(jnp.where(lower, spread, 0.0)), 0.0)
    weights = scores[..., None] * decay * step_part[:, None, :, :]
    within = jnp.einsum("sijh,sjhp->sihp", weights, inner_part, precision=high)
    carried = (
        jnp.einsum("sin,shpn->sihp", c_part, state, precision=high) * jnp.exp(cumul)[..., None]
    )
    tail = jnp.exp(cumul[:, -1:, :] - cumul) * step_part
    fresh = jnp.einsum("sjn,sjh,sjhp->shpn", b_part, tail, inner_part, precision=high)
    new_state = jnp.exp(cumul[:, -1, :])[:, :, None, None] * state + fresh
    return (new_state, within + carried)


def state_space(inner, step, rate, b_mat, c_mat):
    batch, length, heads, head_size = inner.shape
    blocks = length // BLOCK_LEN

    def blockify(values):
        return jnp.moveaxis(values.reshape((batch, blocks, BLOCK_LEN) + values.shape[2:]), 1, 0)

    start = jnp.zeros((batch, heads, head_size, b_mat.shape[2]), dtype=inner.dtype)
    _, outputs = lax.scan(
        jax.checkpoint(block_step),
        start,
        (blockify(inner), blockify(step), blockify(rate), blockify(b_mat), blockify(c_mat)),
    )
    return jnp.moveaxis(outputs, 0, 1).reshape(batch, length, heads, head_size)


def mixer(gate_inner, shared, step_raw, conv_local, conv_common, head_local):
    batch, length = (gate_inner.shape[0], gate_inner.shape[1])
    heads = step_raw.shape[2]
    parts = gate_inner.reshape(batch, length, heads, 2, P_SIZE)
    gate_vals = parts[:, :, :, 0, :].reshape(batch, length, heads * P_SIZE)
    inner_vals = parts[:, :, :, 1, :].reshape(batch, length, heads * P_SIZE)
    inner_act = jax.nn.silu(causal_conv(inner_vals, conv_local))
    shared_act = jax.nn.silu(causal_conv(shared, conv_common))
    half = shared.shape[2] // 2
    step = jax.nn.softplus(step_raw + head_local[0])
    rate = -step * jnp.exp(head_local[1])
    inner_heads = inner_act.reshape(batch, length, heads, P_SIZE)
    output = state_space(inner_heads, step, rate, shared_act[..., :half], shared_act[..., half:])
    output = output + head_local[2][:, None] * inner_heads
    return output.reshape(batch, length, heads * P_SIZE) * jax.nn.silu(gate_vals)


def adamw(param, grad, first, second_moment, rate, decay):
    first_new = beta_one * first + (1.0 - beta_one) * grad
    second_new = beta_two * second_moment + (1.0 - beta_two) * grad * grad
    corrected = (
        first_new
        / (1.0 - beta_one**adam_step)
        / (jnp.sqrt(second_new / (1.0 - beta_two**adam_step)) + adam_eps)
    )
    return (param - rate * (corrected + decay * param), first_new, second_new)


def local(
    block_in,
    cotangent,
    in_weight,
    out_weight,
    in_gain,
    out_gain,
    conv_inner,
    conv_shared,
    head_params,
    first_in_weight,
    first_out_weight,
    first_in_gain,
    first_out_gain,
    first_conv_inner,
    first_conv_shared,
    first_head_params,
    second_in_weight,
    second_out_weight,
    second_in_gain,
    second_out_gain,
    second_conv_inner,
    second_conv_shared,
    second_head_params,
):
    seq_index = lax.axis_index("seq")
    inputs = block_in.astype(jnp.float32)
    rms_in = lax.rsqrt(jnp.mean(inputs * inputs, axis=-1, keepdims=True) + norm_eps)
    normed = (inputs * rms_in * in_gain).astype(jnp.bfloat16)
    in_w16 = in_weight.astype(jnp.bfloat16)
    out_w16 = out_weight.astype(jnp.bfloat16)
    column_list = normed
    projected = jnp.einsum(
        "fbe,ek->fbk",
        column_list,
        lax.all_gather(in_w16, ("seq", "wshard"), axis=0, tiled=True),
        preferred_element_type=jnp.float32,
    ).astype(jnp.bfloat16)
    gate_inner = projected[:, :, : 2 * E]
    shared = projected[:, :, 2 * E : 2 * E + 2 * N_STATE]
    step_raw = projected[:, :, 2 * E + 2 * N_STATE :]
    head_gate, head_step = (
        lax.all_to_all(gate_inner, "seq", split_axis=2, concat_axis=1, tiled=True),
        lax.all_to_all(step_raw, "seq", split_axis=2, concat_axis=1, tiled=True),
    )
    head_shared = lax.all_gather(shared, "seq", axis=1, tiled=True)
    heads_dev = head_step.shape[2]
    inner_start = seq_index * (heads_dev * P_SIZE)
    conv_local = lax.dynamic_slice_in_dim(conv_inner, inner_start, heads_dev * P_SIZE, 1)
    head_local = lax.dynamic_slice_in_dim(head_params, seq_index * heads_dev, heads_dev, 1)
    gated, mixer_back = jax.vjp(
        mixer,
        head_gate.astype(jnp.float32),
        head_shared.astype(jnp.float32),
        head_step.astype(jnp.float32),
        conv_local,
        conv_shared,
        head_local,
    )
    gated32 = lax.all_to_all(
        gated.astype(jnp.bfloat16), "seq", split_axis=1, concat_axis=2, tiled=True
    ).astype(jnp.float32)
    rms_out = lax.rsqrt(jnp.mean(gated32 * gated32, axis=-1, keepdims=True) + norm_eps)
    gnormed = (gated32 * rms_out * out_gain).astype(jnp.bfloat16)
    column_list = gnormed
    mixed = jnp.einsum(
        "brg,ga->bra",
        column_list,
        lax.all_gather(out_w16, ("seq", "wshard"), axis=0, tiled=True),
        preferred_element_type=jnp.float32,
    )
    d_gnormed = jnp.einsum(
        "oum,am->oua",
        cotangent,
        lax.all_gather(out_w16, ("seq", "wshard"), axis=0, tiled=True),
        preferred_element_type=jnp.float32,
    )
    block_out = inputs + mixed
    d_out_gain = jnp.sum(d_gnormed * gated32 * rms_out, axis=(0, 1))
    scaled = d_gnormed * out_gain
    d_gated = (
        rms_out * scaled - gated32 * rms_out**3 * jnp.mean(scaled * gated32, axis=-1, keepdims=True)
    ).astype(jnp.bfloat16)
    head_cotan = lax.all_to_all(d_gated, "seq", split_axis=2, concat_axis=1, tiled=True).astype(
        jnp.float32
    )
    d_gate, d_shared, d_step, d_conv_local, d_common, d_head_local = mixer_back(head_cotan)
    tok_gate, tok_step = (
        lax.all_to_all(d_gate.astype(jnp.bfloat16), "seq", split_axis=1, concat_axis=2, tiled=True),
        lax.all_to_all(d_step.astype(jnp.bfloat16), "seq", split_axis=1, concat_axis=2, tiled=True),
    )
    shared_sum = lax.psum_scatter(
        d_shared.astype(jnp.bfloat16), "seq", scatter_dimension=1, tiled=True
    )
    projected_gradient = jnp.concatenate([tok_gate, shared_sum, tok_step], axis=2)
    d_normed = jnp.einsum(
        "ozu,hu->ozh",
        projected_gradient,
        lax.all_gather(in_w16, ("seq", "wshard"), axis=0, tiled=True),
        preferred_element_type=jnp.float32,
    )
    d_in_gain = jnp.sum(d_normed * inputs * rms_in, axis=(0, 1))
    scaled_in = d_normed * in_gain
    grad_in = (
        cotangent.astype(jnp.float32)
        + rms_in * scaled_in
        - inputs * rms_in**3 * jnp.mean(scaled_in * inputs, axis=-1, keepdims=True)
    )
    d_conv_full = lax.dynamic_update_slice_in_dim(
        jnp.zeros_like(conv_inner), d_conv_local, inner_start, 1
    )
    d_head_full = lax.dynamic_update_slice_in_dim(
        jnp.zeros_like(head_params), d_head_local, seq_index * heads_dev, 1
    )
    grad_in_gain, grad_out_gain, grad_conv_inner, grad_conv_shared, grad_head_params = lax.psum(
        (d_in_gain, d_out_gain, d_conv_full, d_common, d_head_full), ("seq", "wshard")
    )
    column_list = normed
    grad_in_weight = lax.psum_scatter(
        jnp.einsum(
            "nkm,nkc->mc", column_list, projected_gradient, preferred_element_type=jnp.float32
        ),
        ("seq", "wshard"),
        scatter_dimension=0,
        tiled=True,
    )
    column_list = gnormed
    grad_out_weight = lax.psum_scatter(
        jnp.einsum("kcb,kch->bh", column_list, cotangent, preferred_element_type=jnp.float32),
        ("seq", "wshard"),
        scatter_dimension=0,
        tiled=True,
    )
    new_in_weight, new_first_in_weight, new_second_in_weight = adamw(
        in_weight,
        grad_in_weight,
        first_in_weight,
        second_in_weight,
        weight_learning_rate,
        matrix_decay,
    )
    new_out_weight, new_first_out_weight, new_second_out_weight = adamw(
        out_weight,
        grad_out_weight,
        first_out_weight,
        second_out_weight,
        weight_learning_rate,
        matrix_decay,
    )
    updated_input_gain, new_first_in_gain, new_second_in_gain = adamw(
        in_gain, grad_in_gain, first_in_gain, second_in_gain, small_rate, 0.0
    )
    new_out_gain, new_first_out_gain, new_second_out_gain = adamw(
        out_gain, grad_out_gain, first_out_gain, second_out_gain, small_rate, 0.0
    )
    new_conv_inner, new_first_conv_inner, new_second_conv_inner = adamw(
        conv_inner, grad_conv_inner, first_conv_inner, second_conv_inner, small_rate, 0.0
    )
    new_conv_shared, new_first_conv_shared, new_second_conv_shared = adamw(
        conv_shared, grad_conv_shared, first_conv_shared, second_conv_shared, small_rate, 0.0
    )
    new_head_params, updated_head_first_moment, head_second_all = adamw(
        head_params, grad_head_params, first_head_params, second_head_params, small_rate, 0.0
    )
    return (
        block_out,
        grad_in,
        grad_in_weight,
        grad_out_weight,
        grad_in_gain,
        grad_out_gain,
        grad_conv_inner,
        grad_conv_shared,
        grad_head_params,
        new_in_weight,
        new_out_weight,
        updated_input_gain,
        new_out_gain,
        new_conv_inner,
        new_conv_shared,
        new_head_params,
        new_first_in_weight,
        new_first_out_weight,
        new_first_in_gain,
        new_first_out_gain,
        new_first_conv_inner,
        new_first_conv_shared,
        updated_head_first_moment,
        new_second_in_weight,
        new_second_out_weight,
        new_second_in_gain,
        new_second_out_gain,
        new_second_conv_inner,
        new_second_conv_shared,
        head_second_all[0:2],
        head_second_all[2],
    )


def solution(mesh):
    return jax.shard_map(
        local,
        mesh=mesh,
        in_specs=(
            P("wshard", "seq", None),
            P("wshard", "seq", None),
            P(("seq", "wshard"), None),
            P(("seq", "wshard"), None),
            P(),
            P(),
            P(),
            P(),
            P(),
            P(("seq", "wshard"), None),
            P(("seq", "wshard"), None),
            P(),
            P(),
            P(),
            P(),
            P(),
            P(("seq", "wshard"), None),
            P(("seq", "wshard"), None),
            P(),
            P(),
            P(),
            P(),
            P(),
        ),
        out_specs=(
            P("wshard", "seq", None),
            P("wshard", "seq", None),
            P(("seq", "wshard"), None),
            P(("seq", "wshard"), None),
            P(),
            P(),
            P(),
            P(),
            P(),
            P(("seq", "wshard"), None),
            P(("seq", "wshard"), None),
            P(),
            P(),
            P(),
            P(),
            P(),
            P(("seq", "wshard"), None),
            P(("seq", "wshard"), None),
            P(),
            P(),
            P(),
            P(),
            P(),
            P(("seq", "wshard"), None),
            P(("seq", "wshard"), None),
            P(),
            P(),
            P(),
            P(),
            P(),
            P(),
        ),
        check_vma=False,
    )
```

profile of v0, /device:TPU:0, one launch (start us, length us, event | category | flops | bytes accessed | tf_op | source)
XLA Modules:
  0.0 2023.6 jit_solution(13329375079531035761)
XLA Ops:
  11.6 132.1 %all-gather.4.cloned.1.call-done = bf16[1536,6448]{1,0:T(8,128)(2,1)} async-done(((bf16[48,6448]{1,0:T(8,128)(2,1)}), bf16[1536,6448]{1,0:T(8,128)(2,1)}) %all-gather.4.cloned.1.call-update) | async-done | bytes 19808272 | tf_op jit(solution)/shard_map/all_gather | solution.py:130
  143.6 14.0 fusion.107
  167.6 37.2 %copy.613 = bf16[1,256,6144]{1,0,2:T(2,128)(2,1)} copy(bf16[1,256,6144]{1,2,0:T(8,128)(2,1)S(1)} %slice.200) | data formatting | bytes 6291456 | tf_op jit(solution)/shard_map/slice | solution.py:133
  204.9 31.5 %reduce.89 = bf16[6144,256]{1,0:T(8,128)(2,1)S(1)} reduce(bf16[6144,1,256]{2,1,0:T(2,128)(2,1)} %bitcast.657, bf16[]{:T(256)} %broadcast.1020), dimensions={1}, to_apply=%bitcast.470.reduce_sub_computation | reduce | bytes 6291458
  240.0 4.6 all-to-all-start.1
  259.4 23.1 %all-to-all-done.1 = bf16[8,2,98304]{2,1,0:T(2,128)(2,1)S(1)} async-done(((bf16[8,2,98304]{2,1,0:T(2,128)(2,1)}), bf16[8,2,98304]{2,1,0:T(2,128)(2,1)S(1)}, u32[]{:S(2)}, u32[]{:S(2)}) %all-to-all-start.1) | async-done | bytes 3145760 | tf_op jit(solution)/shard_map/all_to_all | solution.py:137
  282.4 5.3 reshape.1694
  287.7 9.1 copy.611
  296.8 7.1 reshape.1633
  307.2 4.5 fusion.118
  317.7 185.0 %while.44 = (s32[]{:T(128)}, f32[1,6,64,128]{3,2,1,0:T(8,128)S(1)}, f32[8,1,256,6,64]{2,0,4,3,1:T(8,128)}, f32[8,1,6,64,128]{4,3,2,1,0:T(8,128)}, f32[8,1,256,6]...) while((s32[]{:T(128)}, f32[1,6,64,128]{3,2,1,0:T(8,128)S(1)}, ...), condition=%wide.region_4.5_spmd.clone.clone, body=%wide.region_1.4_spmd.clone.clone.sunk | while | flops 707349504 | bytes 5805416 | solution.py:59
  331.4 9.8 dynamic_update_slice.95
  354.5 9.8 dynamic_update_slice.95
  377.6 9.8 dynamic_update_slice.95
  400.6 9.8 dynamic_update_slice.95
  423.7 9.8 dynamic_update_slice.95
  446.7 9.8 dynamic_update_slice.95
  469.8 9.8 dynamic_update_slice.95
  492.8 9.8 dynamic_update_slice.95
  502.7 4.6 transpose.193
  507.3 4.8 multiply_convert_fusion.1
  512.0 8.5 copy.488
  520.5 35.5 %reduce.90 = bf16[2048,384]{1,0:T(8,128)(2,1)} reduce(bf16[2048,1,384]{2,1,0:T(2,128)(2,1)} %bitcast.669, bf16[]{:T(256)} %broadcast.1020), dimensions={1}, to_apply=%bitcast.432.reduce_sub_computation | reduce | bytes 3145730
  559.7 4.3 all-to-all-start.2
  564.1 20.9 %all-to-all-done.2 = bf16[8,2,49152]{2,1,0:T(2,128)(2,1)} async-done(((bf16[8,2,49152]{2,1,0:T(2,128)(2,1)}), bf16[8,2,49152]{2,1,0:T(2,128)(2,1)}, u32[]{:S(2)}, u32[]{:S(2)}) %all-to-all-start.2) | async-done | bytes 1572896 | tf_op jit(solution)/shard_map/all_to_all | solution.py:154
  585.1 6.5 reshape.1696
  600.2 10.7 fusion.139
  610.9 204.3 %reduce-scatter.8.cloned.1.call-done = f32[96,1536]{1,0:T(8,128)} async-done(((f32[3072,1536]{1,0:T(8,128)}), f32[96,1536]{1,0:T(8,128)}) %reduce-scatter.8.cloned.1.call-update) | async-done | bytes 589840 | tf_op jit(solution)/shard_map/reduce_scatter | solution.py:222
  822.5 76.8 %all-gather.8.cloned.1.call-done = bf16[3072,1536]{1,0:T(8,128)(2,1)} async-done(((bf16[96,1536]{1,0:T(8,128)(2,1)}), bf16[3072,1536]{1,0:T(8,128)(2,1)}) %all-gather.8.cloned.1.call-update) | async-done | bytes 9437200 | tf_op jit(solution)/shard_map/all_gather | solution.py:163
  899.3 8.4 multiply_reduce_fusion.7
  910.0 7.6 copy.491
  917.6 17.8 reduce.91
  947.2 17.2 all-to-all-done.3
  964.4 4.7 reshape.1698
  981.4 355.6 %while.43 = (s32[]{:T(128)}, f32[1,6,64,128]{3,2,1,0:T(8,128)S(1)}, f32[8,1,256,6,64]{2,0,4,3,1:T(8,128)}, f32[8,1,256,6]{3,2,1,0:T(8,128)}, f32[8,1,256,6]{2,0,...) while((s32[]{:T(128)}, f32[1,6,64,128]{3,2,1,0:T(8,128)S(1)}, ...), condition=%wide.region_19.20_spmd.clone, body=%wide.region_7.19_spmd.clone.sunk | while | flops 1670419456 | bytes 15714059 | solution.py:59
  999.2 9.8 dynamic_update_slice.91
  1009.9 7.6 reduce-window.74
  1043.6 9.8 dynamic_update_slice.91
  1054.3 7.6 reduce-window.74
  1088.0 9.8 dynamic_update_slice.91
  1098.7 7.6 reduce-window.74
  1132.4 9.8 dynamic_update_slice.91
  1143.1 7.6 reduce-window.74
  1176.8 9.8 dynamic_update_slice.91
  1187.5 7.6 reduce-window.74
  1221.2 9.8 dynamic_update_slice.91
  1231.9 7.6 reduce-window.74
  1265.6 9.8 dynamic_update_slice.91
  1276.3 7.6 reduce-window.74
  1310.0 9.8 dynamic_update_slice.91
  1320.7 7.6 reduce-window.74
  1341.8 11.5 reduce.92
  1358.1 4.8 transpose.194
  1369.0 12.4 multiply_reduce_fusion.6
  1392.1 15.7 copy.509
  1407.8 31.6 %reduce.93 = bf16[2048,768]{1,0:T(8,128)(2,1)S(1)} reduce(bf16[2048,1,768]{2,1,0:T(2,128)(2,1)} %bitcast.656, bf16[]{:T(256)} %broadcast.1020), dimensions={1}, to_apply=%bitcast.438.reduce_sub_computation | reduce | bytes 6291458
  1443.0 4.7 all-to-all-start.4
  1460.7 27.7 %all-to-all-done.4 = bf16[8,2,98304]{2,1,0:T(2,128)(2,1)} async-done(((bf16[8,2,98304]{2,1,0:T(2,128)(2,1)}), bf16[8,2,98304]{2,1,0:T(2,128)(2,1)}, u32[]{:S(2)}, u32[]{:S(2)}) %all-to-all-start.4) | async-done | bytes 3145760 | tf_op jit(solution)/shard_map/all_to_all | solution.py:183
  1488.4 7.8 reshape.1702
  1502.4 12.5 fusion.132
  1515.0 18.5 fusion.135
  1535.5 7.8 convert_add_fusion
  1545.1 94.3 %all-reduce.32.cloned.1.call-done = (f32[1536]{0:T(1024)}, f32[3072]{0:T(1024)}, f32[5,3072]{1,0:T(8,128)}, f32[5,256]{1,0:T(8,128)}, f32[3,48]{1,0:T(4,128)}) async-done(((f32[1536]{0:T(1024)}, f32[3072]{0:T(1024)}, f32[5,3072]{1,0:T(8,128)}, f32[5,256]{1,0:T(8,128)}, f32[3,48]{1,0:T(4,128)}), (f32[1536]{0:T(1024)}, f32[3072]{0:T(1024)}, f32[5,3072]{1,0:T(8,128)}, f32[5,256]{1,0:T(8,128)}, ...) | async-done | bytes 85584 | tf_op jit(solution)/shard_map/psum | solution.py:209
  1647.4 361.7 %reduce-scatter.6.cloned.1.call-done = f32[48,6448]{1,0:T(8,128)} async-done(((f32[1536,6448]{1,0:T(8,128)}), f32[48,6448]{1,0:T(8,128)}) %reduce-scatter.6.cloned.1.call-update) | async-done | bytes 1238032 | tf_op jit(solution)/shard_map/reduce_scatter | solution.py:213
  (923 shorter events, 474.9 us)
Async XLA Ops:
  7.2 136.4 %copy-start.11 = (bf16[1,256,1536]{2,1,0:T(8,128)(2,1)S(1)}, bf16[1,256,1536]{2,1,0:T(8,128)(2,1)}, u32[]{:S(2)}) copy-start(bf16[1,256,1536]{2,1,0:T(8,128)(2,1)} %param.27) | copy-start | bytes 2359300
  7.2 136.4 %copy-start.26 = (f32[1536]{0:T(1024)S(1)}, f32[1536]{0:T(1024)}, u32[]{:S(2)}) copy-start(f32[1536]{0:T(1024)} %param.31) | copy-start | bytes 18436
  7.2 136.4 %all-gather.4.cloned.1.call-start = ((), (), s32[]{:S(2)}) async-start(), calls=%async_computation.9 | async-start | bytes 20680704 | tf_op jit(solution)/shard_map/all_gather | solution.py:130
  9.6 238.6 %all-gather.6.cloned.1.call-start = ((), (), s32[]{:S(2)}) async-start(), calls=%async_computation.10 | async-start | bytes 1179648 | tf_op jit(solution)/shard_map/all_gather | solution.py:140
  11.6 146.1 %copy-start.48 = (f32[256]{0:T(256)}, f32[256]{0:T(256)S(1)}, u32[]{:S(2)}) copy-start(f32[256]{0:T(256)S(1)} %get-tuple-element.934) | copy-start | bytes 3076
  162.0 78.0 %all-to-all-start = ((bf16[8,2,768]{2,1,0:T(2,128)(2,1)}), bf16[8,2,768]{2,1,0:T(2,128)(2,1)S(1)}, u32[]{:S(2)}, u32[]{:S(2)}) async-start(bf16[8,2,768]{2,1,0:T(2,128)(2,1)} %reshape.1691), calls=%async_computation | async-start | bytes 49152 | tf_op jit(solution)/shard_map/all_to_all | solution.py:138
  240.0 42.4 %all-to-all-start.1 = ((bf16[8,2,98304]{2,1,0:T(2,128)(2,1)}), bf16[8,2,98304]{2,1,0:T(2,128)(2,1)S(1)}, u32[]{:S(2)}, u32[]{:S(2)}) async-start(bf16[8,2,98304]{2,1,0:T(2,128)(2,1)} %reshape.1693), calls=%async_computation.1 | async-start | bytes 6291456 | tf_op jit(solution)/shard_map/all_to_all | solution.py:137
  244.9 262.4 %copy-start.46 = (f32[384]{0:T(512)}, f32[384]{0:T(512)S(1)}, u32[]{:S(2)}) copy-start(f32[384]{0:T(512)S(1)} %mul.1143) | copy-start | bytes 4612
  245.9 61.3 %copy-start.38 = (f32[384]{0:T(512)}, f32[384]{0:T(512)S(1)}, u32[]{:S(2)}) copy-start(f32[384]{0:T(512)S(1)} %get-tuple-element.804) | copy-start | bytes 4612
  245.9 61.3 %copy-start.40 = (f32[384]{0:T(512)}, f32[384]{0:T(512)S(1)}, u32[]{:S(2)}) copy-start(f32[384]{0:T(512)S(1)} %get-tuple-element.805) | copy-start | bytes 4612
  245.9 61.3 %copy-start.42 = (f32[384]{0:T(512)}, f32[384]{0:T(512)S(1)}, u32[]{:S(2)}) copy-start(f32[384]{0:T(512)S(1)} %get-tuple-element.806) | copy-start | bytes 4612
  245.9 61.3 %copy-start.44 = (f32[384]{0:T(512)}, f32[384]{0:T(512)S(1)}, u32[]{:S(2)}) copy-start(f32[384]{0:T(512)S(1)} %get-tuple-element.807) | copy-start | bytes 4612
  307.2 636.9 %copy-start = (f32[1,2048,6,1,64]{1,4,3,2,0:T(8,128)}, f32[1,2048,6,1,64]{1,4,3,2,0:T(8,128)S(1)}, u32[]{:S(2)}) copy-start(f32[1,2048,6,1,64]{1,4,3,2,0:T(8,128)S(1)} %get-tuple-element.912) | copy-start | bytes 9437188
  559.7 25.3 %all-to-all-start.2 = ((bf16[8,2,49152]{2,1,0:T(2,128)(2,1)}), bf16[8,2,49152]{2,1,0:T(2,128)(2,1)}, u32[]{:S(2)}, u32[]{:S(2)}) async-start(bf16[8,2,49152]{2,1,0:T(2,128)(2,1)} %reshape.1695), calls=%async_computation.2 | async-start | bytes 3145728 | tf_op jit(solution)/shard_map/all_to_all | solution.py:154
  564.1 251.1 %reduce-scatter.8.cloned.1.call-start = ((), (), s32[]{:S(2)}) async-start(), calls=%async_computation.14 | async-start | bytes 19464192 | tf_op jit(solution)/shard_map/reduce_scatter | solution.py:222
  595.9 311.8 %copy-start.60 = (f32[256]{0:T(256)}, f32[256]{0:T(256)S(1)}, u32[]{:S(2)}) copy-start(f32[256]{0:T(256)S(1)} %get-tuple-element.936) | copy-start | bytes 3076
  610.9 288.4 %all-gather.8.cloned.1.call-start = ((), (), s32[]{:S(2)}) async-start(), calls=%async_computation.11 | async-start | bytes 9732096 | tf_op jit(solution)/shard_map/all_gather | solution.py:163
  939.1 25.3 %all-to-all-start.3 = ((bf16[8,2,49152]{2,1,0:T(2,128)(2,1)}), bf16[8,2,49152]{2,1,0:T(2,128)(2,1)}, u32[]{:S(2)}, u32[]{:S(2)}) async-start(bf16[8,2,49152]{2,1,0:T(2,128)(2,1)} %reshape.1697), calls=%async_computation.3 | async-start | bytes 3145728 | tf_op jit(solution)/shard_map/all_to_all | solution.py:178
  996.4 12.7 copy-start.24
  998.7 27.5 %copy-start.14 = (f32[1,6,64,128]{3,2,1,0:T(8,128)S(1)}, f32[1,6,64,128]{3,2,1,0:T(8,128)}, u32[]{:S(2)}) copy-start(f32[1,6,64,128]{3,2,1,0:T(8,128)} %fusion.229) | copy-start | bytes 589828 | tf_op jit(solution)/shard_map/transpose(jvp())/while
  1040.8 12.7 copy-start.24
  1043.1 27.5 %copy-start.14 = (f32[1,6,64,128]{3,2,1,0:T(8,128)S(1)}, f32[1,6,64,128]{3,2,1,0:T(8,128)}, u32[]{:S(2)}) copy-start(f32[1,6,64,128]{3,2,1,0:T(8,128)} %fusion.229) | copy-start | bytes 589828 | tf_op jit(solution)/shard_map/transpose(jvp())/while
  1085.2 12.7 copy-start.24
  1087.5 27.5 %copy-start.14 = (f32[1,6,64,128]{3,2,1,0:T(8,128)S(1)}, f32[1,6,64,128]{3,2,1,0:T(8,128)}, u32[]{:S(2)}) copy-start(f32[1,6,64,128]{3,2,1,0:T(8,128)} %fusion.229) | copy-start | bytes 589828 | tf_op jit(solution)/shard_map/transpose(jvp())/while
  1129.6 12.7 copy-start.24
  1131.9 27.5 %copy-start.14 = (f32[1,6,64,128]{3,2,1,0:T(8,128)S(1)}, f32[1,6,64,128]{3,2,1,0:T(8,128)}, u32[]{:S(2)}) copy-start(f32[1,6,64,128]{3,2,1,0:T(8,128)} %fusion.229) | copy-start | bytes 589828 | tf_op jit(solution)/shard_map/transpose(jvp())/while
  1174.0 12.7 copy-start.24
  1176.3 27.5 %copy-start.14 = (f32[1,6,64,128]{3,2,1,0:T(8,128)S(1)}, f32[1,6,64,128]{3,2,1,0:T(8,128)}, u32[]{:S(2)}) copy-start(f32[1,6,64,128]{3,2,1,0:T(8,128)} %fusion.229) | copy-start | bytes 589828 | tf_op jit(solution)/shard_map/transpose(jvp())/while
  1218.4 12.7 copy-start.24
  1220.8 27.5 %copy-start.14 = (f32[1,6,64,128]{3,2,1,0:T(8,128)S(1)}, f32[1,6,64,128]{3,2,1,0:T(8,128)}, u32[]{:S(2)}) copy-start(f32[1,6,64,128]{3,2,1,0:T(8,128)} %fusion.229) | copy-start | bytes 589828 | tf_op jit(solution)/shard_map/transpose(jvp())/while
  1262.8 12.7 copy-start.24
  1265.2 27.5 %copy-start.14 = (f32[1,6,64,128]{3,2,1,0:T(8,128)S(1)}, f32[1,6,64,128]{3,2,1,0:T(8,128)}, u32[]{:S(2)}) copy-start(f32[1,6,64,128]{3,2,1,0:T(8,128)} %fusion.229) | copy-start | bytes 589828 | tf_op jit(solution)/shard_map/transpose(jvp())/while
  1307.2 12.7 copy-start.24
  1309.6 27.5 %copy-start.14 = (f32[1,6,64,128]{3,2,1,0:T(8,128)S(1)}, f32[1,6,64,128]{3,2,1,0:T(8,128)}, u32[]{:S(2)}) copy-start(f32[1,6,64,128]{3,2,1,0:T(8,128)} %fusion.229) | copy-start | bytes 589828 | tf_op jit(solution)/shard_map/transpose(jvp())/while
  1354.7 88.3 %all-to-all-start.5 = ((bf16[8,2,768]{2,1,0:T(2,128)(2,1)}), bf16[8,2,768]{2,1,0:T(2,128)(2,1)S(1)}, u32[]{:S(2)}, u32[]{:S(2)}) async-start(bf16[8,2,768]{2,1,0:T(2,128)(2,1)} %reshape.1699), calls=%async_computation.6 | async-start | bytes 49152 | tf_op jit(solution)/shard_map/all_to_all | solution.py:184
  1369.0 12.4 copy-start.41
  1443.0 45.4 %all-to-all-start.4 = ((bf16[8,2,98304]{2,1,0:T(2,128)(2,1)}), bf16[8,2,98304]{2,1,0:T(2,128)(2,1)}, u32[]{:S(2)}, u32[]{:S(2)}) async-start(bf16[8,2,98304]{2,1,0:T(2,128)(2,1)} %reshape.1701), calls=%async_computation.4 | async-start | bytes 6291456 | tf_op jit(solution)/shard_map/all_to_all | solution.py:183
  1447.7 54.6 %reduce-scatter.4.cloned.1.call-start = ((), (), s32[]{:S(2)}) async-start(), calls=%async_computation.12 | async-start | bytes 1179648 | tf_op jit(solution)/shard_map/reduce_scatter | solution.py:186
  1455.5 184.0 %all-reduce.32.cloned.1.call-start = ((), (), s32[]{:S(2)}) async-start(), calls=%async_computation.15 | async-start | bytes 258048 | tf_op jit(solution)/shard_map/psum | solution.py:209
  1458.2 38.1 %copy-start.66 = (f32[3,48]{1,0:T(4,128)}, f32[3,48]{1,0:T(4,128)S(1)}, u32[]{:S(2)}) copy-start(f32[3,48]{1,0:T(4,128)S(1)} %dynamic_update_slice.68) | copy-start | bytes 1732
  1458.8 37.4 %copy-start.20 = (f32[5,3072]{1,0:T(8,128)}, f32[5,3072]{1,0:T(8,128)S(1)}, u32[]{:S(2)}) copy-start(f32[5,3072]{1,0:T(8,128)S(1)} %add_dynamic-update-slice_fusion) | copy-start | bytes 184324
  1502.4 12.6 copy-start.9
  1502.4 12.6 copy-start.25
  1514.9 494.2 %reduce-scatter.6.cloned.1.call-start = ((), (), s32[]{:S(2)}) async-start(), calls=%async_computation.13 | async-start | bytes 41361408 | tf_op jit(solution)/shard_map/reduce_scatter | solution.py:213
  1543.3 96.2 %copy-start.72 = (f32[3,48]{1,0:T(4,128)S(1)}, f32[3,48]{1,0:T(4,128)}, u32[]{:S(2)}) copy-start(f32[3,48]{1,0:T(4,128)} %param.35) | copy-start | bytes 1732
  1543.3 96.2 %copy-start.77 = (f32[3,48]{1,0:T(4,128)S(1)}, f32[3,48]{1,0:T(4,128)}, u32[]{:S(2)}) copy-start(f32[3,48]{1,0:T(4,128)} %param.42) | copy-start | bytes 1732
  1543.3 96.2 %copy-start.78 = (f32[3,48]{1,0:T(4,128)S(1)}, f32[3,48]{1,0:T(4,128)}, u32[]{:S(2)}) copy-start(f32[3,48]{1,0:T(4,128)} %param.49) | copy-start | bytes 1732
  1543.3 98.4 %copy-start.67 = (f32[1536]{0:T(1024)S(1)}, f32[1536]{0:T(1024)}, u32[]{:S(2)}) copy-start(f32[1536]{0:T(1024)} %param.38) | copy-start | bytes 18436
  1543.3 98.4 %copy-start.68 = (f32[1536]{0:T(1024)S(1)}, f32[1536]{0:T(1024)}, u32[]{:S(2)}) copy-start(f32[1536]{0:T(1024)} %param.45) | copy-start | bytes 18436
  1543.3 99.8 %copy-start.37 = (f32[5,256]{1,0:T(8,128)S(1)}, f32[5,256]{1,0:T(8,128)}, u32[]{:S(2)}) copy-start(f32[5,256]{1,0:T(8,128)} %param.34) | copy-start | bytes 15364
  1543.3 99.7 %copy-start.69 = (f32[5,256]{1,0:T(8,128)S(1)}, f32[5,256]{1,0:T(8,128)}, u32[]{:S(2)}) copy-start(f32[5,256]{1,0:T(8,128)} %param.41) | copy-start | bytes 15364
  1543.3 99.7 %copy-start.70 = (f32[5,256]{1,0:T(8,128)S(1)}, f32[5,256]{1,0:T(8,128)}, u32[]{:S(2)}) copy-start(f32[5,256]{1,0:T(8,128)} %param.48) | copy-start | bytes 15364
  1543.3 101.0 %copy-start.50 = (f32[3072]{0:T(1024)S(1)}, f32[3072]{0:T(1024)}, u32[]{:S(2)}) copy-start(f32[3072]{0:T(1024)} %param.39) | copy-start | bytes 36868
  1543.4 101.0 %copy-start.51 = (f32[3072]{0:T(1024)S(1)}, f32[3072]{0:T(1024)}, u32[]{:S(2)}) copy-start(f32[3072]{0:T(1024)} %param.46) | copy-start | bytes 36868
  1543.4 102.4 %copy-start.28 = (f32[5,3072]{1,0:T(8,128)S(1)}, f32[5,3072]{1,0:T(8,128)}, u32[]{:S(2)}) copy-start(f32[5,3072]{1,0:T(8,128)} %param.33) | copy-start | bytes 184324
  1543.4 102.4 %copy-start.31 = (f32[5,3072]{1,0:T(8,128)S(1)}, f32[5,3072]{1,0:T(8,128)}, u32[]{:S(2)}) copy-start(f32[5,3072]{1,0:T(8,128)} %param.40) | copy-start | bytes 184324
  1543.4 102.3 %copy-start.32 = (f32[5,3072]{1,0:T(8,128)S(1)}, f32[5,3072]{1,0:T(8,128)}, u32[]{:S(2)}) copy-start(f32[5,3072]{1,0:T(8,128)} %param.47) | copy-start | bytes 184324
  1543.4 465.7 %copy-start.13 = (f32[48,6448]{1,0:T(8,128)S(1)}, f32[48,6448]{1,0:T(8,128)}, u32[]{:S(2)}) copy-start(f32[48,6448]{1,0:T(8,128)} %param.29) | copy-start | bytes 3714052
  1543.4 465.7 %copy-start.18 = (f32[48,6448]{1,0:T(8,128)S(1)}, f32[48,6448]{1,0:T(8,128)}, u32[]{:S(2)}) copy-start(f32[48,6448]{1,0:T(8,128)} %param.36) | copy-start | bytes 3714052
  1647.4 365.9 %copy-start.35 = (f32[1536]{0:T(1024)S(1)}, f32[1536]{0:T(1024)}, u32[]{:S(2)}) copy-start(f32[1536]{0:T(1024)} %get-tuple-element.1242) | copy-start | bytes 18436
  1647.4 366.5 %copy-start.33 = (f32[3072]{0:T(1024)S(1)}, f32[3072]{0:T(1024)}, u32[]{:S(2)}) copy-start(f32[3072]{0:T(1024)} %get-tuple-element.1243) | copy-start | bytes 36868
  1647.4 367.1 %copy-start.21 = (f32[5,3072]{1,0:T(8,128)S(1)}, f32[5,3072]{1,0:T(8,128)}, u32[]{:S(2)}) copy-start(f32[5,3072]{1,0:T(8,128)} %get-tuple-element.1244) | copy-start | bytes 184324
  1647.4 367.8 %copy-start.34 = (f32[5,256]{1,0:T(8,128)S(1)}, f32[5,256]{1,0:T(8,128)}, u32[]{:S(2)}) copy-start(f32[5,256]{1,0:T(8,128)} %get-tuple-element.1245) | copy-start | bytes 15364
  1647.4 368.4 %copy-start.73 = (f32[3,48]{1,0:T(4,128)S(1)}, f32[3,48]{1,0:T(4,128)}, u32[]{:S(2)}) copy-start(f32[3,48]{1,0:T(4,128)} %get-tuple-element.1246) | copy-start | bytes 1732
  (56 other events, 249.7 us)
Sparse Core Ops, SparseCore 0:
  11.4 132.1 all-gather.3
  159.4 21.6 all-gather.5
  611.0 204.1 reduce-scatter.7
  818.7 80.5 all-gather.7
  1455.6 38.7 reduce-scatter.3
  1515.0 124.3 all-reduce.31
  1646.4 362.6 reduce-scatter.5
where the time goes:
time: 2040 us; the launch traced here: 2020 us
  waiting for transfers between devices  958 us (47%)
  local copies, waits for them, and re-layouts  484 us (24%)
  other arithmetic  326 us (16%)
  matrix products  211 us (10%)
  starting transfers between devices  25.1 us (1%)
    reduce_scatter x1, waiting for transfers between devices, local(): lax.psum_scatter(jnp.einsum('nkm,nkc->mc', column_list, projected_gradien...  362 us
    dynamic_update_slice x56, local copies, waits for them, and re-layouts, state_space(): lax.scan(jax.checkpoint(block_step), start, (blockify(inner), blockify(st...  215 us
    reduce_scatter x1, waiting for transfers between devices, local(): lax.psum_scatter(jnp.einsum('kcb,kch->bh', column_list, cotangent, prefer...  204 us
    all_gather x1, waiting for transfers between devices, local(): lax.all_gather(in_w16, ('seq', 'wshard'), axis=0, tiled=True)  132 us
    unnamed x10, other arithmetic  132 us
    psum x1, waiting for transfers between devices, local(): lax.psum((d_in_gain, d_out_gain, d_conv_full, d_common, d_head_full), ('s...  94.3 us
    another operation x49, other arithmetic  93.2 us
    all_gather x1, waiting for transfers between devices, local(): lax.all_gather(out_w16, ('seq', 'wshard'), axis=0, tiled=True)  76.8 us
  transfers between devices with their start and end apart: 13, of which 9 were waited for; matrix products, arithmetic and copies ran while one was open for 12% of the time, Pallas kernels for 0%

commit v1 on v0

--- a/solution.py
+++ b/solution.py
@@ -1,3 +1,4 @@
+import functools
 import jax
 import jax.numpy as jnp
 from jax import lax
@@ -15,6 +16,29 @@
 weight_learning_rate = 0.01
 matrix_decay = 0.1
 small_rate = 0.1
+
+
+def _cover_cycles(page, shard_axis):
+    earlier = lax.axis_size(shard_axis)
+    local_now, found_now, r1 = (earlier, lax.axis_index(shard_axis), page.shape[0])
+    small, piece_out = (page, 1)
+    while piece_out < local_now:
+        small = jnp.concatenate(
+            [
+                small,
+                lax.ppermute(
+                    small,
+                    shard_axis,
+                    [(dev, (dev - piece_out) % local_now) for dev in range(local_now)],
+                ),
+            ],
+            axis=0,
+        )
+        piece_out = 2 * piece_out
+    return jnp.roll(small, found_now * r1, axis=0)
+
+
+order_task = functools.partial(_cover_cycles, shard_axis=("seq", "wshard"))
 
 
 def causal_conv(values, taps):
@@ -125,10 +149,7 @@
     out_w16 = out_weight.astype(jnp.bfloat16)
     column_list = normed
     projected = jnp.einsum(
-        "fbe,ek->fbk",
-        column_list,
-        lax.all_gather(in_w16, ("seq", "wshard"), axis=0, tiled=True),
-        preferred_element_type=jnp.float32,
+        "fbe,ek->fbk", column_list, order_task(in_w16), preferred_element_type=jnp.float32
     ).astype(jnp.bfloat16)
     gate_inner = projected[:, :, : 2 * E]
     shared = projected[:, :, 2 * E : 2 * E + 2 * N_STATE]

time: 2040 us -> 2520 us (1.24)
  waiting for transfers between devices: 958 us -> 1240 us
  local copies, waits for them, and re-layouts: 484 us -> 609 us
  matrix products: 211 us -> 252 us
    ppermute x0 -> x5, waiting for transfers between devices: none -> 407 us  [_cover_cycles(): lax.ppermute(small, shard_axis, [(dev, (dev - piece_out) % local_now) for...]
    all_gather x1, waiting for transfers between devices: 132 us -> 0.01 us  [local(): lax.all_gather(in_w16, ('seq', 'wshard'), axis=0, tiled=True)]
    concatenate x0 -> x3, local copies, waits for them, and re-layouts: none -> 90.1 us  [the longest x1 64.8 us: _cover_cycles(): return jnp.roll(small, found_now * r1, axis=0)]
    unnamed x177 -> x183, local copies, waits for them, and re-layouts: 69 us -> 73.8 us
  transfers between devices with their start and end apart: 13 -> 18, of which waited for: 9 -> 13; matrix products, arithmetic and copies ran while one was open for 12% -> 29% of each run, Pallas kernels for 0% -> 0%
where the time goes in v1:
time: 2520 us; the launch traced here: 2500 us
  waiting for transfers between devices  1240 us (49%)
  local copies, waits for them, and re-layouts  609 us (24%)
  other arithmetic  344 us (14%)
  matrix products  252 us (10%)
  starting transfers between devices  39 us (2%)
    ppermute x5, waiting for transfers between devices, _cover_cycles(): lax.ppermute(small, shard_axis, [(dev, (dev - piece_out) % local_now) for...  407 us
    reduce_scatter x1, waiting for transfers between devices, local(): lax.psum_scatter(jnp.einsum('nkm,nkc->mc', column_list, projected_gradien...  362 us
    dynamic_update_slice x56, local copies, waits for them, and re-layouts, state_space(): lax.scan(jax.checkpoint(block_step), start, (blockify(inner), blockify(st...  215 us
    reduce_scatter x1, waiting for transfers between devices, local(): lax.psum_scatter(jnp.einsum('kcb,kch->bh', column_list, cotangent, prefer...  205 us
    unnamed x10, other arithmetic  133 us
    psum x1, waiting for transfers between devices, local(): lax.psum((d_in_gain, d_out_gain, d_conv_full, d_common, d_head_full), ('s...  94.2 us
    another operation x49, other arithmetic  93.2 us
    dot_general x24, matrix products, block_step(): within = jnp.einsum('sijh,sjhp->sihp', weights, inner_part, precision=high)  83.5 us
  transfers between devices with their start and end apart: 18, of which 13 were waited for; matrix products, arithmetic and copies ran while one was open for 29% of the time, Pallas kernels for 0%

profile of v1, /device:TPU:0, one launch (start us, length us, event | category | flops | bytes accessed | tf_op | source)
XLA Modules:
  0.0 2500.8 jit_solution(2325882373690745529)
XLA Ops:
  8.6 6.5 collective-permute-start
  15.1 12.6 collective-permute-done
  29.2 54.1 %collective-permute-done.1 = bf16[96,6448]{1,0:T(8,128)(2,1)S(1)} collective-permute-done((bf16[96,6448]{1,0:T(8,128)(2,1)S(1)}, bf16[96,6448]{1,0:T(8,128)(2,1)S(1)}, u32[]{:S(2)}, u32[]{:S(2)}) %collective-permute-start.1) | collective-permute-done | bytes 1238048 | tf_op jit(solution)/shard_map/ppermute | solution.py:29
  86.8 27.9 %collective-permute-done.2 = bf16[192,6448]{1,0:T(8,128)(2,1)S(1)} collective-permute-done((bf16[192,6448]{1,0:T(8,128)(2,1)S(1)}, bf16[192,6448]{1,0:T(8,128)(2,1)S(1)}, u32[]{:S(2)}, u32[]{:S(2)}) %collective-permute-start.2) | collective-permute-done | bytes 2476064 | tf_op jit(solution)/shard_map/ppermute | solution.py:29
  119.2 7.6 copy.520
  136.6 99.7 %collective-permute-done.3 = bf16[384,6448]{0,1:T(8,128)(2,1)} collective-permute-done((bf16[384,6448]{0,1:T(8,128)(2,1)}, bf16[384,6448]{0,1:T(8,128)(2,1)}, u32[]{:S(2)}, u32[]{:S(2)}) %collective-permute-start.3) | collective-permute-done | bytes 4952096 | tf_op jit(solution)/shard_map/ppermute | solution.py:29
  236.3 17.7 concatenate.28
  256.3 212.4 %collective-permute-done.4 = bf16[768,6448]{0,1:T(8,128)(2,1)} collective-permute-done((bf16[768,6448]{0,1:T(8,128)(2,1)}, bf16[768,6448]{0,1:T(8,128)(2,1)}, u32[]{:S(2)}, u32[]{:S(2)}) %collective-permute-start.4) | collective-permute-done | bytes 9904160 | tf_op jit(solution)/shard_map/ppermute | solution.py:29
  468.8 64.8 %concatenate.29 = bf16[3072,6448]{0,1:T(8,128)(2,1)} concatenate(bf16[48,6448]{0,1:T(8,128)(2,1)} %copy.525, bf16[48,6448]{0,1:T(8,128)(2,1)} %copy.526, bf16[96,6448]{0,1:T(8,128)(2,1)} %copy.527, bf16[192,6448]{0,1:T(8,128)(2,1)S(1)} %copy.528, bf16[384,6448]{0,1:T(8,128)(2,1)} %collective-permute-done.3, bf16[768,6448]{0,1:T(8,128)(2,1)} %collective-permute-done.4, ...), dimensions={0} | concatenate | bytes 79233024 | tf_op jit(solution)/shard_map/jit(_roll_dynamic)/concatenate | solution.py:38
  533.6 14.1 fusion.112
  555.2 37.2 %copy.667 = bf16[1,256,6144]{1,0,2:T(2,128)(2,1)} copy(bf16[1,256,6144]{1,2,0:T(8,128)(2,1)S(1)} %slice.200) | data formatting | bytes 6291456 | tf_op jit(solution)/shard_map/slice | solution.py:154
  592.4 31.5 %reduce.89 = bf16[6144,256]{1,0:T(8,128)(2,1)S(1)} reduce(bf16[6144,1,256]{2,1,0:T(2,128)(2,1)} %bitcast.656, bf16[]{:T(256)} %broadcast.1020), dimensions={1}, to_apply=%bitcast.469.reduce_sub_computation | reduce | bytes 6291458
  646.8 23.1 all-to-all-done.1
  675.3 9.1 copy.665
  684.4 7.1 reshape.1633
  705.3 192.1 %while.44 = (s32[]{:T(128)}, f32[1,6,64,128]{3,2,1,0:T(8,128)S(1)}, f32[8,1,256,6,64]{2,0,4,3,1:T(8,128)}, f32[8,1,6,64,128]{4,3,2,1,0:T(8,128)}, f32[8,1,256,6]...) while((s32[]{:T(128)}, f32[1,6,64,128]{3,2,1,0:T(8,128)S(1)}, ...), condition=%wide.region_4.5_spmd.clone.clone, body=%wide.region_1.4_spmd.clone.clone.sunk | while | flops 707349504 | bytes 5806421 | solution.py:83
  717.5 9.8 dynamic_update_slice.95
  741.4 9.8 dynamic_update_slice.95
  765.4 9.8 dynamic_update_slice.95
  789.4 9.8 dynamic_update_slice.95
  813.3 9.8 dynamic_update_slice.95
  837.3 9.8 dynamic_update_slice.95
  861.3 9.8 dynamic_update_slice.95
  885.2 9.8 dynamic_update_slice.95
  906.7 8.5 copy.542
  915.2 35.4 %reduce.90 = bf16[2048,384]{1,0:T(8,128)(2,1)} reduce(bf16[2048,1,384]{2,1,0:T(2,128)(2,1)} %bitcast.668, bf16[]{:T(256)} %broadcast.1020), dimensions={1}, to_apply=%bitcast.432.reduce_sub_computation | reduce | bytes 3145730
  958.7 20.9 all-to-all-done.2
  979.6 6.5 reshape.1696
  994.8 10.7 fusion.146
  1005.5 205.4 %reduce-scatter.8.cloned.1.call-done = f32[96,1536]{1,0:T(8,128)} async-done(((f32[3072,1536]{1,0:T(8,128)}), f32[96,1536]{1,0:T(8,128)}) %reduce-scatter.8.cloned.1.call-update) | async-done | bytes 589840 | tf_op jit(solution)/shard_map/reduce_scatter | solution.py:243
  1218.2 76.9 %all-gather.6.cloned.1.call-done = bf16[3072,1536]{1,0:T(8,128)(2,1)} async-done(((bf16[96,1536]{1,0:T(8,128)(2,1)}), bf16[3072,1536]{1,0:T(8,128)(2,1)}) %all-gather.6.cloned.1.call-update) | async-done | bytes 9437200 | tf_op jit(solution)/shard_map/all_gather | solution.py:184
  1295.2 8.4 multiply_reduce_fusion.7
  1305.9 7.6 copy.545
  1313.5 17.7 reduce.91
  1343.6 21.1 all-to-all-done.3
  1364.7 6.3 reshape.1698
  1383.9 433.3 %while.43 = (s32[]{:T(128)}, f32[1,6,64,128]{3,2,1,0:T(8,128)S(1)}, f32[8,1,256,6,64]{2,0,4,3,1:T(8,128)}, f32[8,1,256,6]{3,2,1,0:T(8,128)}, f32[8,1,256,6]{2,0,...) while((s32[]{:T(128)}, f32[1,6,64,128]{3,2,1,0:T(8,128)S(1)}, ...), condition=%wide.region_19.20_spmd.clone, body=%wide.region_7.19_spmd.clone.sunk | while | flops 1670419456 | bytes 15190127 | solution.py:83
  1415.5 7.6 reduce-window.74
  1427.9 9.9 dynamic_update_slice.91
  1469.7 7.6 reduce-window.74
  1482.1 9.8 dynamic_update_slice.91
  1523.8 7.6 reduce-window.74
  1536.2 9.8 dynamic_update_slice.91
  1577.9 7.6 reduce-window.74
  1590.3 9.8 dynamic_update_slice.91
  1632.0 7.6 reduce-window.74
  1644.5 9.8 dynamic_update_slice.91
  1686.2 7.6 reduce-window.74
  1698.6 9.8 dynamic_update_slice.91
  1740.3 7.6 reduce-window.74
  1752.7 9.8 dynamic_update_slice.91
  1794.4 7.6 reduce-window.74
  1806.8 9.8 dynamic_update_slice.91
  1833.3 13.3 reduce.92
  1852.6 12.1 multiply_reduce_fusion.6
  1868.9 11.3 copy.563
  1880.2 31.6 %reduce.93 = bf16[2048,768]{1,0:T(8,128)(2,1)S(1)} reduce(bf16[2048,1,768]{2,1,0:T(2,128)(2,1)} %bitcast.655, bf16[]{:T(256)} %broadcast.1020), dimensions={1}, to_apply=%bitcast.438.reduce_sub_computation | reduce | bytes 6291458
  1937.9 27.8 %all-to-all-done.4 = bf16[8,2,98304]{2,1,0:T(2,128)(2,1)} async-done(((bf16[8,2,98304]{2,1,0:T(2,128)(2,1)}), bf16[8,2,98304]{2,1,0:T(2,128)(2,1)}, u32[]{:S(2)}, u32[]{:S(2)}) %all-to-all-start.4) | async-done | bytes 3145760 | tf_op jit(solution)/shard_map/all_to_all | solution.py:204
  1965.6 7.8 reshape.1702
  1979.7 12.5 fusion.139
  1992.3 18.5 fusion.142
  2012.8 7.8 convert_add_fusion
  2022.4 94.2 %all-reduce.32.cloned.1.call-done = (f32[1536]{0:T(1024)}, f32[3072]{0:T(1024)}, f32[5,3072]{1,0:T(8,128)}, f32[5,256]{1,0:T(8,128)}, f32[3,48]{1,0:T(4,128)}) async-done(((f32[1536]{0:T(1024)}, f32[3072]{0:T(1024)}, f32[5,3072]{1,0:T(8,128)}, f32[5,256]{1,0:T(8,128)}, f32[3,48]{1,0:T(4,128)}), (f32[1536]{0:T(1024)}, f32[3072]{0:T(1024)}, f32[5,3072]{1,0:T(8,128)}, f32[5,256]{1,0:T(8,128)}, ...) | async-done | bytes 85584 | tf_op jit(solution)/shard_map/psum | solution.py:230
  2124.7 361.7 %reduce-scatter.6.cloned.1.call-done = f32[48,6448]{1,0:T(8,128)} async-done(((f32[1536,6448]{1,0:T(8,128)}), f32[48,6448]{1,0:T(8,128)}) %reduce-scatter.6.cloned.1.call-update) | async-done | bytes 1238032 | tf_op jit(solution)/shard_map/reduce_scatter | solution.py:234
  (933 shorter events, 615.3 us)
Async XLA Ops:
  7.2 628.5 %all-gather.4.cloned.1.call-start = ((), (), s32[]{:S(2)}) async-start(), calls=%async_computation.9 | async-start | bytes 1179648 | tf_op jit(solution)/shard_map/all_gather | solution.py:161
  8.6 119.2 %copy-start.3 = (bf16[48,6448]{1,0:T(8,128)(2,1)}, bf16[48,6448]{1,0:T(8,128)(2,1)S(1)}, u32[]{:S(2)}) copy-start(bf16[48,6448]{1,0:T(8,128)(2,1)S(1)} %convert_element_type.220) | copy-start | bytes 1857028
  8.6 19.1 collective-permute-start
  27.8 55.5 %collective-permute-start.1 = (bf16[96,6448]{1,0:T(8,128)(2,1)S(1)}, bf16[96,6448]{1,0:T(8,128)(2,1)S(1)}, u32[]{:S(2)}, u32[]{:S(2)}) collective-permute-start(bf16[96,6448]{1,0:T(8,128)(2,1)S(1)} %pad_maximum_fusion.2), channel_id=1, source_target_pairs={{0,30},{1,31},{2,0},{3,1},{4,2},{5,3},{6,4},{7,5},{8,6},{9,7},{10,... | collective-permute-start | bytes 3714056 | tf_op jit(solution)/shard_map/ppermute | solution.py:29
  83.5 31.2 %collective-permute-start.2 = (bf16[192,6448]{1,0:T(8,128)(2,1)S(1)}, bf16[192,6448]{1,0:T(8,128)(2,1)S(1)}, u32[]{:S(2)}, u32[]{:S(2)}) collective-permute-start(bf16[192,6448]{1,0:T(8,128)(2,1)S(1)} %pad_maximum_fusion.1), channel_id=1, source_target_pairs={{0,28},{1,29},{2,30},{3,31},{4,0},{5,1},{6,2},{7,3},{8,4},{9,5},{1... | collective-permute-start | bytes 7428104 | tf_op jit(solution)/shard_map/ppermute | solution.py:29
  126.7 109.5 %collective-permute-start.3 = (bf16[384,6448]{0,1:T(8,128)(2,1)}, bf16[384,6448]{0,1:T(8,128)(2,1)}, u32[]{:S(2)}, u32[]{:S(2)}) collective-permute-start(bf16[384,6448]{0,1:T(8,128)(2,1)} %copy.520), channel_id=1, source_target_pairs={{0,24},{1,25},{2,26},{3,27},{4,28},{5,29},{6,30},{7,31},{8,0},{9,1... | collective-permute-start | bytes 14856200 | tf_op jit(solution)/shard_map/ppermute | solution.py:29
  254.0 214.8 %collective-permute-start.4 = (bf16[768,6448]{0,1:T(8,128)(2,1)}, bf16[768,6448]{0,1:T(8,128)(2,1)}, u32[]{:S(2)}, u32[]{:S(2)}) collective-permute-start(bf16[768,6448]{0,1:T(8,128)(2,1)} %concatenate.28), channel_id=1, source_target_pairs={{0,16},{1,17},{2,18},{3,19},{4,20},{5,21},{6,22},{7,23},{8,24},{9,... | collective-permute-start | bytes 29712392 | tf_op jit(solution)/shard_map/ppermute | solution.py:29
  256.3 277.2 %copy-start.50 = (f32[256]{0:T(256)}, f32[256]{0:T(256)S(1)}, u32[]{:S(2)}) copy-start(f32[256]{0:T(256)S(1)} %get-tuple-element.934) | copy-start | bytes 3076
  256.3 277.2 %copy-start.28 = (f32[1536]{0:T(1024)S(1)}, f32[1536]{0:T(1024)}, u32[]{:S(2)}) copy-start(f32[1536]{0:T(1024)} %param.31) | copy-start | bytes 18436
  550.4 77.2 %all-to-all-start = ((bf16[8,2,768]{2,1,0:T(2,128)(2,1)}), bf16[8,2,768]{2,1,0:T(2,128)(2,1)S(1)}, u32[]{:S(2)}, u32[]{:S(2)}) async-start(bf16[8,2,768]{2,1,0:T(2,128)(2,1)} %reshape.1691), calls=%async_computation | async-start | bytes 49152 | tf_op jit(solution)/shard_map/all_to_all | solution.py:159
  627.6 42.4 %all-to-all-start.1 = ((bf16[8,2,98304]{2,1,0:T(2,128)(2,1)}), bf16[8,2,98304]{2,1,0:T(2,128)(2,1)S(1)}, u32[]{:S(2)}, u32[]{:S(2)}) async-start(bf16[8,2,98304]{2,1,0:T(2,128)(2,1)} %reshape.1693), calls=%async_computation.1 | async-start | bytes 6291456 | tf_op jit(solution)/shard_map/all_to_all | solution.py:158
  632.2 8.1 copy-start.64
  632.2 8.1 copy-start.66
  632.4 269.5 %copy-start.48 = (f32[384]{0:T(512)}, f32[384]{0:T(512)S(1)}, u32[]{:S(2)}) copy-start(f32[384]{0:T(512)S(1)} %mul.1151) | copy-start | bytes 4612
  633.4 61.4 %copy-start.40 = (f32[384]{0:T(512)}, f32[384]{0:T(512)S(1)}, u32[]{:S(2)}) copy-start(f32[384]{0:T(512)S(1)} %get-tuple-element.804) | copy-start | bytes 4612
  633.4 61.4 %copy-start.42 = (f32[384]{0:T(512)}, f32[384]{0:T(512)S(1)}, u32[]{:S(2)}) copy-start(f32[384]{0:T(512)S(1)} %get-tuple-element.805) | copy-start | bytes 4612
  633.4 61.4 %copy-start.44 = (f32[384]{0:T(512)}, f32[384]{0:T(512)S(1)}, u32[]{:S(2)}) copy-start(f32[384]{0:T(512)S(1)} %get-tuple-element.806) | copy-start | bytes 4612
  633.4 61.4 %copy-start.46 = (f32[384]{0:T(512)}, f32[384]{0:T(512)S(1)}, u32[]{:S(2)}) copy-start(f32[384]{0:T(512)S(1)} %get-tuple-element.807) | copy-start | bytes 4612
  634.1 705.7 %copy-start.19 = (bf16[48,1,256]{2,1,0:T(2,128)(2,1)}, bf16[48,1,256]{2,1,0:T(2,128)(2,1)S(1)}, u32[]{:S(2)}) copy-start(bf16[48,1,256]{2,1,0:T(2,128)(2,1)S(1)} %reshape.1692) | copy-start | bytes 73732
  694.7 645.8 %copy-start = (f32[1,2048,6,1,64]{1,4,3,2,0:T(8,128)}, f32[1,2048,6,1,64]{1,4,3,2,0:T(8,128)S(1)}, u32[]{:S(2)}) copy-start(f32[1,2048,6,1,64]{1,4,3,2,0:T(8,128)S(1)} %get-tuple-element.912) | copy-start | bytes 9437188
  950.6 8.1 copy-start.31
  954.3 25.3 %all-to-all-start.2 = ((bf16[8,2,49152]{2,1,0:T(2,128)(2,1)}), bf16[8,2,49152]{2,1,0:T(2,128)(2,1)}, u32[]{:S(2)}, u32[]{:S(2)}) async-start(bf16[8,2,49152]{2,1,0:T(2,128)(2,1)} %reshape.1695), calls=%async_computation.2 | async-start | bytes 3145728 | tf_op jit(solution)/shard_map/all_to_all | solution.py:175
  958.6 252.3 %reduce-scatter.8.cloned.1.call-start = ((), (), s32[]{:S(2)}) async-start(), calls=%async_computation.14 | async-start | bytes 19464192 | tf_op jit(solution)/shard_map/reduce_scatter | solution.py:243
  990.5 313.1 %copy-start.62 = (f32[256]{0:T(256)}, f32[256]{0:T(256)S(1)}, u32[]{:S(2)}) copy-start(f32[256]{0:T(256)S(1)} %get-tuple-element.936) | copy-start | bytes 3076
  1005.5 289.7 %all-gather.6.cloned.1.call-start = ((), (), s32[]{:S(2)}) async-start(), calls=%async_computation.10 | async-start | bytes 9732096 | tf_op jit(solution)/shard_map/all_gather | solution.py:184
  1295.2 8.4 copy-start.6
  1334.9 29.8 %all-to-all-start.3 = ((bf16[8,2,49152]{2,1,0:T(2,128)(2,1)}), bf16[8,2,49152]{2,1,0:T(2,128)(2,1)}, u32[]{:S(2)}, u32[]{:S(2)}) async-start(bf16[8,2,49152]{2,1,0:T(2,128)(2,1)} %reshape.1697), calls=%async_computation.3 | async-start | bytes 3145728 | tf_op jit(solution)/shard_map/all_to_all | solution.py:199
  1339.2 640.4 %all-gather.8.cloned.1.call-start = ((), (), s32[]{:S(2)}) async-start(), calls=%async_computation.12 | async-start | bytes 20680704 | tf_op jit(solution)/shard_map/all_gather | solution.py:214
  1829.0 23.6 copy-start.1
  1829.0 23.6 copy-start.49
  1849.1 71.2 %all-to-all-start.5 = ((bf16[8,2,768]{2,1,0:T(2,128)(2,1)}), bf16[8,2,768]{2,1,0:T(2,128)(2,1)S(1)}, u32[]{:S(2)}, u32[]{:S(2)}) async-start(bf16[8,2,768]{2,1,0:T(2,128)(2,1)} %reshape.1699), calls=%async_computation.6 | async-start | bytes 49152 | tf_op jit(solution)/shard_map/all_to_all | solution.py:205
  1852.6 12.2 copy-start.41
  1852.6 12.2 copy-start.43
  1852.6 12.2 copy-start.45
  1852.6 12.2 copy-start.47
  1920.2 45.4 %all-to-all-start.4 = ((bf16[8,2,98304]{2,1,0:T(2,128)(2,1)}), bf16[8,2,98304]{2,1,0:T(2,128)(2,1)}, u32[]{:S(2)}, u32[]{:S(2)}) async-start(bf16[8,2,98304]{2,1,0:T(2,128)(2,1)} %reshape.1701), calls=%async_computation.4 | async-start | bytes 6291456 | tf_op jit(solution)/shard_map/all_to_all | solution.py:204
  1925.0 54.7 %reduce-scatter.4.cloned.1.call-start = ((), (), s32[]{:S(2)}) async-start(), calls=%async_computation.11 | async-start | bytes 1179648 | tf_op jit(solution)/shard_map/reduce_scatter | solution.py:207
  1932.7 184.0 %all-reduce.32.cloned.1.call-start = ((), (), s32[]{:S(2)}) async-start(), calls=%async_computation.15 | async-start | bytes 258048 | tf_op jit(solution)/shard_map/psum | solution.py:230
  1935.3 38.1 %copy-start.68 = (f32[3,48]{1,0:T(4,128)}, f32[3,48]{1,0:T(4,128)S(1)}, u32[]{:S(2)}) copy-start(f32[3,48]{1,0:T(4,128)S(1)} %dynamic_update_slice.68) | copy-start | bytes 1732
  1936.0 37.5 %copy-start.22 = (f32[5,3072]{1,0:T(8,128)}, f32[5,3072]{1,0:T(8,128)S(1)}, u32[]{:S(2)}) copy-start(f32[5,3072]{1,0:T(8,128)S(1)} %add_dynamic-update-slice_fusion) | copy-start | bytes 184324
  1979.7 12.6 copy-start.9
  1979.7 12.6 copy-start.27
  1992.2 494.1 %reduce-scatter.6.cloned.1.call-start = ((), (), s32[]{:S(2)}) async-start(), calls=%async_computation.13 | async-start | bytes 41361408 | tf_op jit(solution)/shard_map/reduce_scatter | solution.py:234
  2012.7 8.0 copy-start.17
  2020.6 96.1 %copy-start.74 = (f32[3,48]{1,0:T(4,128)S(1)}, f32[3,48]{1,0:T(4,128)}, u32[]{:S(2)}) copy-start(f32[3,48]{1,0:T(4,128)} %param.35) | copy-start | bytes 1732
  2020.6 96.1 %copy-start.79 = (f32[3,48]{1,0:T(4,128)S(1)}, f32[3,48]{1,0:T(4,128)}, u32[]{:S(2)}) copy-start(f32[3,48]{1,0:T(4,128)} %param.42) | copy-start | bytes 1732
  2020.6 96.1 %copy-start.80 = (f32[3,48]{1,0:T(4,128)S(1)}, f32[3,48]{1,0:T(4,128)}, u32[]{:S(2)}) copy-start(f32[3,48]{1,0:T(4,128)} %param.49) | copy-start | bytes 1732
  2020.6 98.4 %copy-start.39 = (f32[5,256]{1,0:T(8,128)S(1)}, f32[5,256]{1,0:T(8,128)}, u32[]{:S(2)}) copy-start(f32[5,256]{1,0:T(8,128)} %param.34) | copy-start | bytes 15364
  2020.6 98.4 %copy-start.69 = (f32[5,256]{1,0:T(8,128)S(1)}, f32[5,256]{1,0:T(8,128)}, u32[]{:S(2)}) copy-start(f32[5,256]{1,0:T(8,128)} %param.41) | copy-start | bytes 15364
  2020.6 98.4 %copy-start.70 = (f32[5,256]{1,0:T(8,128)S(1)}, f32[5,256]{1,0:T(8,128)}, u32[]{:S(2)}) copy-start(f32[5,256]{1,0:T(8,128)} %param.48) | copy-start | bytes 15364
  2020.6 99.7 %copy-start.71 = (f32[1536]{0:T(1024)S(1)}, f32[1536]{0:T(1024)}, u32[]{:S(2)}) copy-start(f32[1536]{0:T(1024)} %param.38) | copy-start | bytes 18436
  2020.6 99.7 %copy-start.72 = (f32[1536]{0:T(1024)S(1)}, f32[1536]{0:T(1024)}, u32[]{:S(2)}) copy-start(f32[1536]{0:T(1024)} %param.45) | copy-start | bytes 18436
  2020.6 101.0 %copy-start.52 = (f32[3072]{0:T(1024)S(1)}, f32[3072]{0:T(1024)}, u32[]{:S(2)}) copy-start(f32[3072]{0:T(1024)} %param.39) | copy-start | bytes 36868
  2020.7 101.0 %copy-start.53 = (f32[3072]{0:T(1024)S(1)}, f32[3072]{0:T(1024)}, u32[]{:S(2)}) copy-start(f32[3072]{0:T(1024)} %param.46) | copy-start | bytes 36868
  2020.7 102.3 %copy-start.30 = (f32[5,3072]{1,0:T(8,128)S(1)}, f32[5,3072]{1,0:T(8,128)}, u32[]{:S(2)}) copy-start(f32[5,3072]{1,0:T(8,128)} %param.33) | copy-start | bytes 184324
  2020.7 102.3 %copy-start.33 = (f32[5,3072]{1,0:T(8,128)S(1)}, f32[5,3072]{1,0:T(8,128)}, u32[]{:S(2)}) copy-start(f32[5,3072]{1,0:T(8,128)} %param.40) | copy-start | bytes 184324
  2020.7 102.3 %copy-start.34 = (f32[5,3072]{1,0:T(8,128)S(1)}, f32[5,3072]{1,0:T(8,128)}, u32[]{:S(2)}) copy-start(f32[5,3072]{1,0:T(8,128)} %param.47) | copy-start | bytes 184324
  2020.7 465.6 %copy-start.13 = (f32[48,6448]{1,0:T(8,128)S(1)}, f32[48,6448]{1,0:T(8,128)}, u32[]{:S(2)}) copy-start(f32[48,6448]{1,0:T(8,128)} %param.29) | copy-start | bytes 3714052
  2020.7 465.6 %copy-start.18 = (f32[48,6448]{1,0:T(8,128)S(1)}, f32[48,6448]{1,0:T(8,128)}, u32[]{:S(2)}) copy-start(f32[48,6448]{1,0:T(8,128)} %param.36) | copy-start | bytes 3714052
  2124.7 365.8 %copy-start.37 = (f32[1536]{0:T(1024)S(1)}, f32[1536]{0:T(1024)}, u32[]{:S(2)}) copy-start(f32[1536]{0:T(1024)} %get-tuple-element.1242) | copy-start | bytes 18436
  2124.7 366.4 %copy-start.35 = (f32[3072]{0:T(1024)S(1)}, f32[3072]{0:T(1024)}, u32[]{:S(2)}) copy-start(f32[3072]{0:T(1024)} %get-tuple-element.1243) | copy-start | bytes 36868
  2124.7 367.1 %copy-start.23 = (f32[5,3072]{1,0:T(8,128)S(1)}, f32[5,3072]{1,0:T(8,128)}, u32[]{:S(2)}) copy-start(f32[5,3072]{1,0:T(8,128)} %get-tuple-element.1244) | copy-start | bytes 184324
  2124.7 367.7 %copy-start.36 = (f32[5,256]{1,0:T(8,128)S(1)}, f32[5,256]{1,0:T(8,128)}, u32[]{:S(2)}) copy-start(f32[5,256]{1,0:T(8,128)} %get-tuple-element.1245) | copy-start | bytes 15364
  2124.7 368.3 %copy-start.75 = (f32[3,48]{1,0:T(4,128)S(1)}, f32[3,48]{1,0:T(4,128)}, u32[]{:S(2)}) copy-start(f32[3,48]{1,0:T(4,128)} %get-tuple-element.1246) | copy-start | bytes 1732
  (56 other events, 216.3 us)
Sparse Core Ops, SparseCore 0:
  548.5 24.1 all-gather.3
  1005.6 205.2 reduce-scatter.7
  1214.5 80.6 all-gather.5
  1342.5 132.7 all-gather.7
  1932.8 38.7 reduce-scatter.3
  1992.3 124.2 all-reduce.31
  2123.6 362.6 reduce-scatter.5
